TPU v7x, 16 devices: a whole 2x2x2 slice. The times are simulated.
16 devices in a mesh: dp: 2 (over z), tp: 8 (over y, x, core).
Axes of the slice: x: 2, y: 2, z: 2, core: 2. Of those that a mesh axis runs over, the one named last changes fastest.
Arguments:
- hidden_in: bfloat16 [2048, 4096], P(('dp', 'tp')), parts along dimension 0
- k_cache: bfloat16 [2048, 512, 256], P(('dp', 'tp')), parts along dimension 0
- v_cache: bfloat16 [2048, 512, 256], P(('dp', 'tp')), parts along dimension 0
- cache_len: int32 [2048], P(('dp', 'tp')), parts along dimension 0
- norm_attn: bfloat16 [4096], replicated
- norm_mlp: bfloat16 [4096], replicated
- w_q: bfloat16 [4096, 4096], replicated
- w_k: bfloat16 [4096, 256], replicated
- w_v: bfloat16 [4096, 256], replicated
- w_o: bfloat16 [4096, 4096], replicated
- w_gate: bfloat16 [4096, 16384], P(None, 'tp')
- w_up: bfloat16 [4096, 16384], P(None, 'tp')
- w_down: bfloat16 [16384, 4096], P('tp')
Outputs:
- output 1: bfloat16 [2048, 4096], P(('dp', 'tp')), parts along dimension 0
- output 2: bfloat16 [2048, 256], P(('dp', 'tp')), parts along dimension 0
- output 3: bfloat16 [2048, 256], P(('dp', 'tp')), parts along dimension 0
There are 2 independent parts. A program takes and returns all parts, laid end to end along the dimension named above; an argument that names none is the same for every part.
All inputs are finite; a program needn't handle non-finite values.
Results may differ from a plain program's by a relative error of at most 0.0059934.
Values are sent between devices in bfloat16 or wider.
A program may use at most 1 GiB of HBM per device.

v0:
```python
import jax
import jax.numpy as jnp
from jax import lax
from jax.sharding import PartitionSpec as P


def rms_scale(values, gain_vec):
    wide_vals = values.astype(jnp.float32)
    inv_rms = lax.rsqrt(jnp.mean(wide_vals * wide_vals, axis=-1, keepdims=True) + 1e-6)
    return (wide_vals * inv_rms * (1.0 + gain_vec.astype(jnp.float32))).astype(jnp.bfloat16)


def rope_tables(positions, head_dim):
    half_dim = head_dim // 2
    inv_freq = 10000.0 ** (-2.0 * jnp.arange(half_dim, dtype=jnp.float32) / head_dim)
    angles = positions.astype(jnp.float32)[:, None] * inv_freq[None, :]
    return jnp.cos(angles), jnp.sin(angles)


def rotary(values, cos_t, sin_t):
    half_dim = values.shape[-1] // 2
    first_half = values[..., :half_dim]
    second_half = values[..., half_dim:]
    return jnp.concatenate([first_half * cos_t - second_half * sin_t, second_half * cos_t + first_half * sin_t], axis=-1)


def attend(q_rot, k_new, v_new, k_cache, v_cache, cache_len):
    hist_score = jnp.einsum('bhd,btd->bht', q_rot, k_cache, preferred_element_type=jnp.float32)
    new_score = jnp.einsum('bhd,bd->bh', q_rot, k_new, preferred_element_type=jnp.float32)
    valid_mask = lax.broadcasted_iota(jnp.int32, (1, 1, k_cache.shape[1]), 2) < cache_len[:, None, None]
    hist_score = jnp.where(valid_mask, hist_score, -jnp.inf)
    peak_score = jnp.maximum(jnp.max(hist_score, axis=-1), new_score)
    hist_weight = jnp.exp(hist_score - peak_score[..., None])
    new_weight = jnp.exp(new_score - peak_score)
    weight_sum = jnp.sum(hist_weight, axis=-1) + new_weight
    hist_prob = (hist_weight / weight_sum[..., None]).astype(jnp.bfloat16)
    new_prob = (new_weight / weight_sum).astype(jnp.bfloat16)
    attn_out = jnp.einsum('bht,btd->bhd', hist_prob, v_cache, preferred_element_type=jnp.float32)
    attn_out = attn_out + new_prob.astype(jnp.float32)[..., None] * v_new.astype(jnp.float32)[:, None, :]
    return attn_out.astype(jnp.bfloat16)


def attention_block(hidden_in, k_cache, v_cache, cache_len, norm_attn, w_q, w_k, w_v, w_o):
    num_rows = hidden_in.shape[0]
    head_dim = w_k.shape[1]
    num_heads = w_q.shape[1] // head_dim
    normed = rms_scale(hidden_in, norm_attn)
    q_lin = jnp.dot(normed, w_q, preferred_element_type=jnp.float32).reshape(num_rows, num_heads, head_dim)
    k_lin = jnp.dot(normed, w_k, preferred_element_type=jnp.float32)
    v_new = jnp.dot(normed, w_v, preferred_element_type=jnp.float32).astype(jnp.bfloat16)
    cos_t, sin_t = rope_tables(cache_len, head_dim)
    q_rot = (rotary(q_lin, cos_t[:, None, :], sin_t[:, None, :]) * head_dim ** -0.5).astype(jnp.bfloat16)
    k_new = rotary(k_lin, cos_t, sin_t).astype(jnp.bfloat16)
    attn_out = attend(q_rot, k_new, v_new, k_cache, v_cache, cache_len)
    mixed = jnp.dot(attn_out.reshape(num_rows, num_heads * head_dim), w_o, preferred_element_type=jnp.float32)
    return hidden_in.astype(jnp.float32) + mixed, k_new, v_new


def solution(mesh):
    row_spec = P(('dp', 'tp'), None)
    cache_spec = P(('dp', 'tp'), None, None)
    full_vec = P(None)
    full_mat = P(None, None)

    def per_device(hidden_in, k_cache, v_cache, cache_len, norm_attn, norm_mlp, w_q, w_k, w_v, w_o, w_gate, w_up, w_down):
        x_mid, k_new, v_new = attention_block(hidden_in, k_cache, v_cache, cache_len, norm_attn, w_q, w_k, w_v, w_o)
        xn_mid = rms_scale(x_mid, norm_mlp)
        group_rows = lax.all_gather(xn_mid, 'tp', axis=0, tiled=True)
        gate_act = jnp.dot(group_rows, w_gate, preferred_element_type=jnp.float32)
        up_act = jnp.dot(group_rows, w_up, preferred_element_type=jnp.float32)
        hidden_act = (jax.nn.gelu(gate_act, approximate=True) * up_act).astype(jnp.bfloat16)
        part_sum = jnp.dot(hidden_act, w_down, preferred_element_type=jnp.float32)
        down_sum = lax.psum_scatter(part_sum, 'tp', scatter_dimension=0, tiled=True)
        return (x_mid + down_sum).astype(jnp.bfloat16), k_new, v_new

    return jax.shard_map(
        per_device,
        mesh=mesh,
        in_specs=(row_spec, cache_spec, cache_spec, P(('dp', 'tp')), full_vec, full_vec,
                  full_mat, full_mat, full_mat, full_mat, P(None, 'tp'), P(None, 'tp'), P('tp', None)),
        out_specs=(row_spec, row_spec, row_spec),
        check_vma=False,
    )
```

profile of v0, /device:TPU:0, one launch (start us, length us, event | category | flops | bytes accessed | tf_op | source)
XLA Modules:
  0.0 325.7 jit_solution(9603282710693374304)
XLA Ops:
  7.2 0.0 all-gather.2.cloned.1.call-start
  7.3 0.8 convert_element_type.50
  8.1 0.8 iota_compare_fusion
  8.9 1.5 fusion.14
  10.4 0.7 convert_add_fusion.1
  11.1 0.7 convert_add_fusion
  11.8 2.4 fusion.39
  14.3 1.1 fusion.43
  15.4 12.9 %fusion.41 = f32[128,4096]{1,0:T(8,128)S(1)} fusion(bf16[4096,4096]{1,0:T(8,128)(2,1)} %param.19, bf16[128,4096]{1,0:T(8,128)(2,1)S(1)} %copy-done.3, f32[4096]{0:T(1024)S(1)} %convert_add_fusion.1, f32[128]{0:T(128)S(1)} %add_rsqrt_fusion.1), kind=kOutput, calls=%fused_computation.65 | convolution fusion | flops 4297064448 | bytes 36717056 | tf_op jit(solution)/shard_map/dot_general | solution.py:48
  28.3 0.7 copy.18
  29.0 0.3 subtract_convert_fusion
  29.4 0.6 copy-done.4
  30.0 0.3 multiply_subtract_fusion
  30.3 0.4 fusion.22
  30.7 16.8 %select_reduce_fusion = (f32[128,16]{1,0:T(8,128)S(1)}, f32[128,16,512]{2,1,0:T(8,128)}) fusion(pred[128,512]{1,0:T(8,128)(4,1)S(1)} %iota_compare_fusion, bf16[128,512,256]{2,1,0:T(8,128)(2,1)} %param.14, f32[128,16,128]{2,1,0:T(8,128)S(1)} %get-tuple-element.4, f32[128,16,128]{2,1,0:T(8,128)S(1)} %get-tuple-element.3), kind=kOutput, calls=%fused_computation.16 | convolution fusion | flops 540538880 | bytes 39919616 | tf_op jit(solution)/shard_map/bhd,btd->bht/dot_general | solution.py:28
  47.4 3.4 %fusion.12 = f32[128,16]{1,0:T(8,128)S(1)} fusion(f32[128,16,512]{2,1,0:T(8,128)} %get-tuple-element.12, f32[128,16]{1,0:T(8,128)S(1)} %max.3, pred[128,512]{1,0:T(8,128)(4,1)S(1)} %iota_compare_fusion), kind=kLoop, calls=%fused_computation.17 | loop fusion | flops 3143680 | bytes 4276224 | tf_op jit(solution)/shard_map/reduce_sum | solution.py:35
  50.9 16.7 %add_convert_fusion.1 = bf16[128,16,256]{2,1,0:T(8,128)(2,1)S(1)} fusion(bf16[128,512,256]{2,1,0:T(8,128)(2,1)} %param.15, f32[128,16,512]{2,1,0:T(8,128)} %get-tuple-element.12, f32[128,16]{1,0:T(8,128)S(1)} %get-tuple-element.6, f32[128,16]{1,0:T(8,128)S(1)} %max.3, pred[128,512]{1,0:T(8,128)(4,1)S(1)} %iota_compare_fusion, ...), kind=kOutput, calls=%fused_computation.29 | convolution fusion | flops 542638080 | bytes 39018496 | tf_op jit(solution)/shard_map/bht,btd->bhd/dot_general | solution.py:38
  67.5 0.4 copy.19
  68.0 13.3 %multiply_reduce_fusion = (f32[128]{0:T(128)S(1)}, f32[128,4096]{1,0:T(8,128)S(1)}) fusion(bf16[128,4096]{1,0:T(8,128)(2,1)S(1)} %bitcast.31, bf16[4096,4096]{1,0:T(8,128)(2,1)} %param.22, bf16[128,4096]{1,0:T(8,128)(2,1)S(1)} %copy-done.3), kind=kOutput, calls=%fused_computation.28 | convolution fusion | flops 4297064448 | bytes 37749248 | tf_op jit(solution)/shard_map/dot_general | solution.py:55
  81.3 1.5 multiply_convert_fusion
  82.8 0.0 all-gather.2.cloned.1.call-update
  82.8 0.0 reduce-scatter.2.cloned.1.call-start
  82.9 53.1 %all-gather.2.cloned.1.call-done = bf16[1024,4096]{1,0:T(8,128)(2,1)} async-done(((bf16[128,4096]{1,0:T(8,128)(2,1)}), bf16[1024,4096]{1,0:T(8,128)(2,1)}) %all-gather.2.cloned.1.call-update) | async-done | bytes 8388624 | tf_op jit(solution)/shard_map/all_gather | solution.py:68
  135.9 24.1 %fusion.44 = f32[1024,2048]{1,0:T(8,128)} fusion(bf16[1024,4096]{1,0:T(8,128)(2,1)} %all-gather.2.cloned.1.call-done, bf16[4096,2048]{1,0:T(8,128)(2,1)} %param.23), kind=kOutput, calls=%fused_computation.67 | convolution fusion | flops 17179869184 | bytes 33554432 | tf_op jit(solution)/shard_map/dot_general | solution.py:69
  160.1 23.7 %fusion.8.clone.4 = bf16[1024,2048]{1,0:T(8,128)(2,1)} fusion(f32[1024,2048]{1,0:T(8,128)} %fusion.44, bf16[1024,4096]{1,0:T(8,128)(2,1)S(1)} %copy-done.8, bf16[4096,2048]{1,0:T(8,128)(2,1)} %param.24), kind=kOutput, calls=%fused_computation.9.clone.clone.clone.1 | convolution fusion | flops 17200840704 | bytes 37748736 | tf_op jit(solution)/shard_map/dot_general | solution.py:70
  183.8 21.8 %fusion.9 = f32[1024,4096]{1,0:T(8,128)} fusion(bf16[2048,4096]{1,0:T(8,128)(2,1)S(1)} %bitcast.35, bf16[1024,2048]{1,0:T(8,128)(2,1)} %fusion.8.clone.4), kind=kOutput, calls=%fused_computation.11 | convolution fusion | flops 17179869184 | bytes 37748736 | tf_op jit(solution)/shard_map/dot_general | solution.py:72
  205.6 0.0 reduce-scatter.2.cloned.1.call-update
  205.6 0.7 copy-done.5
  206.3 0.0 copy-done.7
  206.4 0.6 pad_maximum_fusion
  207.0 108.5 %reduce-scatter.2.cloned.1.call-done = f32[128,4096]{1,0:T(8,128)} async-done(((f32[1024,4096]{1,0:T(8,128)}), f32[128,4096]{1,0:T(8,128)}) %reduce-scatter.2.cloned.1.call-update) | async-done | bytes 2097168 | tf_op jit(solution)/shard_map/reduce_scatter | solution.py:73
  315.5 3.4 %add_convert_fusion = bf16[128,4096]{1,0:T(8,128)(2,1)} fusion(f32[128,4096]{1,0:T(8,128)} %copy-done.2, f32[128,4096]{1,0:T(8,128)} %reduce-scatter.2.cloned.1.call-done), kind=kLoop, calls=%fused_computation.26 | loop fusion | flops 1048576 | bytes 5242880 | tf_op jit(solution)/shard_map/convert_element_type | solution.py:74
  (30 shorter events, 0.1 us)
Async XLA Ops:
  7.2 7.1 %copy-start = (bf16[4096,256]{1,0:T(8,128)(2,1)S(1)}, bf16[4096,256]{1,0:T(8,128)(2,1)}, u32[]{:S(2)}) copy-start(bf16[4096,256]{1,0:T(8,128)(2,1)} %param.21) | copy-start | bytes 6291460
  7.2 7.1 %copy-start.3 = (bf16[128,4096]{1,0:T(8,128)(2,1)S(1)}, bf16[128,4096]{1,0:T(8,128)(2,1)}, u32[]{:S(2)}) copy-start(bf16[128,4096]{1,0:T(8,128)(2,1)} %param.13) | copy-start | bytes 3145732
  7.2 128.8 %all-gather.2.cloned.1.call-start = ((), (), s32[]{:S(2)}) async-start(), calls=%async_computation.1 | async-start | bytes 9437184 | tf_op jit(solution)/shard_map/all_gather | solution.py:68
  29.3 0.6 copy-start.4
  29.4 0.6 copy-start.6
  81.3 78.8 %copy-start.2 = (f32[128,4096]{1,0:T(8,128)}, f32[128,4096]{1,0:T(8,128)S(1)}, u32[]{:S(2)}) copy-start(f32[128,4096]{1,0:T(8,128)S(1)} %get-tuple-element.16) | copy-start | bytes 6291460
  82.8 232.7 %reduce-scatter.2.cloned.1.call-start = ((), (), s32[]{:S(2)}) async-start(), calls=%async_computation.2 | async-start | bytes 18874368 | tf_op jit(solution)/shard_map/reduce_scatter | solution.py:73
  135.9 24.2 %copy-start.8 = (bf16[1024,4096]{1,0:T(8,128)(2,1)S(1)}, bf16[1024,4096]{1,0:T(8,128)(2,1)}, u32[]{:S(2)}) copy-start(bf16[1024,4096]{1,0:T(8,128)(2,1)} %all-gather.2.cloned.1.call-done) | copy-start | bytes 25165828
  135.9 47.8 %slice-start = ((s8[16777216]{0:T(1024)(128)(4,1)}), s8[4194304]{0:T(1024)(128)(4,1)S(1)}, s32[]{:S(2)}) async-start(s8[16777216]{0:T(1024)(128)(4,1)} %bitcast.34), calls=%async_computation.3 | async-start | bytes 8388608
  135.9 47.8 %slice-start.1 = ((s8[16777216]{0:T(1024)(128)(4,1)}), s8[4194304]{0:T(1024)(128)(4,1)S(1)}, s32[]{:S(2)}) async-start(s8[16777216]{0:T(1024)(128)(4,1)} %bitcast.34), calls=%async_computation.4 | async-start | bytes 8388608
  160.1 23.7 %slice-start.2 = ((s8[16777216]{0:T(1024)(128)(4,1)}), s8[4194304]{0:T(1024)(128)(4,1)S(1)}, s32[]{:S(2)}) async-start(s8[16777216]{0:T(1024)(128)(4,1)} %bitcast.34), calls=%async_computation.5 | async-start | bytes 8388608
  160.1 23.7 %slice-start.3 = ((s8[16777216]{0:T(1024)(128)(4,1)}), s8[4194304]{0:T(1024)(128)(4,1)S(1)}, s32[]{:S(2)}) async-start(s8[16777216]{0:T(1024)(128)(4,1)} %bitcast.34), calls=%async_computation.6 | async-start | bytes 8388608
  205.6 0.8 copy-start.5
  205.6 0.8 copy-start.7
  206.4 112.5 %copy-start.1 = (bf16[4096,256]{1,0:T(8,128)(2,1)S(1)}, bf16[4096,256]{1,0:T(8,128)(2,1)}, u32[]{:S(2)}) copy-start(bf16[4096,256]{1,0:T(8,128)(2,1)} %param.21) | copy-start | bytes 6291460
Sparse Core Ops, SparseCore 0:
  82.9 52.9 all-gather.1
  205.7 109.7 reduce-scatter.1
where the time goes:
time: 326 us
  waiting for transfers between devices  162 us (50%)
  matrix products  133 us (41%)
  other arithmetic  14.2 us (4%)
  between operations  14.2 us (4%)
    reduce_scatter x1, waiting for transfers between devices, per_device(): down_sum = lax.psum_scatter(part_sum, 'tp', scatter_dimension=0, tiled=True)  108 us
    all_gather x1, waiting for transfers between devices, per_device(): group_rows = lax.all_gather(xn_mid, 'tp', axis=0, tiled=True)  53.1 us
    dot_general x1, matrix products, per_device(): gate_act = jnp.dot(group_rows, w_gate, preferred_element_type=jnp.float32)  24.1 us
    dot_general x1, matrix products, per_device(): up_act = jnp.dot(group_rows, w_up, preferred_element_type=jnp.float32)  23.7 us
    dot_general x1, matrix products, per_device(): part_sum = jnp.dot(hidden_act, w_down, preferred_element_type=jnp.float32)  21.8 us
    dot_general x1, matrix products, attend(): jnp.einsum('bhd,btd->bht', q_rot, k_cache, preferred_element_type=jnp.flo...  16.8 us
    dot_general x1, matrix products, attend(): jnp.einsum('bht,btd->bhd', hist_prob, v_cache, preferred_element_type=jnp...  16.7 us
    dot_general x1, matrix products, attention_block(): jnp.dot(attn_out.reshape(num_rows, num_heads * head_dim), w_o, preferred_...  13.3 us
  transfers between devices with their start and end apart: 2, of which 2 were waited for; matrix products, arithmetic and copies ran while one was open for 0% of the time, Pallas kernels for 0%

commit v1 on v0

--- a/solution.py
+++ b/solution.py
@@ -1,7 +1,273 @@
+import functools
+
 import jax
 import jax.numpy as jnp
 from jax import lax
+from jax.experimental import pallas as pl
+from jax.experimental.pallas import tpu as pltpu
 from jax.sharding import PartitionSpec as P
+
+ROWS = 128
+PIECE = 64
+SUB = 32
+
+
+def mlp_kernel(num_tp, xn_ref, xmid_ref, wg_hbm, wu_hbm, wd_hbm, out_ref,
+               xg, hid, wg_buf, wu_buf, wd_buf, part, mate_out, mate_in, relay, from_x, from_y,
+               wg_sem, wu_sem, wd_sem, send_sem, recv_sem):
+    me = lax.axis_index('tp')
+    mate = me + 1 - 2 * lax.rem(me, 2)
+    xpeer = me + 2 - 4 * lax.rem(me // 2, 2)
+    ypeer = me + 4 - 8 * (me // 4)
+
+    h_tile = wg_buf.shape[2]
+    n_tile = wd_buf.shape[2]
+    h_steps = hid.shape[1] // h_tile
+    n_steps = wd_hbm.shape[1] // n_tile
+    groups = num_tp // 2
+    gu_slots = wg_buf.shape[0]
+    d_slots = wd_buf.shape[0]
+
+    def gate_copy(step):
+        cols = pl.ds(pl.multiple_of(lax.rem(step, h_steps) * h_tile, h_tile), h_tile)
+        slot = lax.rem(step, gu_slots)
+        return (pltpu.make_async_copy(wg_hbm.at[:, cols], wg_buf.at[slot], wg_sem.at[slot]),
+                pltpu.make_async_copy(wu_hbm.at[:, cols], wu_buf.at[slot], wu_sem.at[slot]))
+
+    def down_copy(step):
+        cols = pl.ds(pl.multiple_of(lax.rem(step, n_steps) * n_tile, n_tile), n_tile)
+        slot = lax.rem(step, d_slots)
+        return pltpu.make_async_copy(wd_hbm.at[:, cols], wd_buf.at[slot], wd_sem.at[slot])
+
+    for step in range(gu_slots):
+        for copy in gate_copy(jnp.int32(step)):
+            copy.start()
+    for step in range(d_slots):
+        down_copy(jnp.int32(step)).start()
+
+    barrier = pltpu.get_barrier_semaphore()
+    for peer in (mate, xpeer, ypeer):
+        pl.semaphore_signal(barrier, inc=1, device_id={'tp': peer}, device_id_type=pl.DeviceIdType.MESH)
+    pl.semaphore_wait(barrier, 3)
+
+    count = [0]
+
+    def remote(src, dst, peer):
+        k = count[0]
+        count[0] += 1
+        return pltpu.make_async_remote_copy(
+            src_ref=src, dst_ref=dst, send_sem=send_sem.at[k], recv_sem=recv_sem.at[k],
+            device_id={'tp': peer}, device_id_type=pl.DeviceIdType.MESH)
+
+    def rows_of(start, size):
+        return xg.at[pl.ds(start, size), :]
+
+    top, bot = xn_ref.at[pl.ds(0, PIECE), :], xn_ref.at[pl.ds(PIECE, PIECE), :]
+    own_mate = remote(xn_ref, rows_of(128, 128), mate)
+    near_x = remote(top, rows_of(256, 64), xpeer)
+    near_y = remote(bot, rows_of(320, 64), ypeer)
+    diag_y = remote(rows_of(256, 64), rows_of(512, 64), ypeer)
+    diag_x = remote(rows_of(320, 64), rows_of(576, 64), xpeer)
+    far_x = remote(bot, rows_of(768, 64), xpeer)
+    far_y = remote(top, rows_of(832, 64), ypeer)
+    near_mate = remote(rows_of(256, 128), rows_of(384, 128), mate)
+    diag_mate = remote(rows_of(512, 128), rows_of(640, 128), mate)
+    far_mate = remote(rows_of(768, 128), rows_of(896, 128), mate)
+    pair_sum = [remote(mate_out.at[g % 2], mate_in.at[g], mate) for g in range(groups)]
+    chunks = range(PIECE // SUB)
+
+    def span(lead, c):
+        return pl.ds(lead + c * SUB, SUB)
+
+    near_sx = [remote(part.at[1, span(0, c), :], from_x.at[span(0, c), :], xpeer) for c in chunks]
+    near_sy = [remote(part.at[1, span(PIECE, c), :], from_y.at[span(PIECE, c), :], ypeer) for c in chunks]
+    diag_sx = [remote(part.at[2, span(0, c), :], relay.at[span(PIECE, c), :], xpeer) for c in chunks]
+    diag_sy = [remote(part.at[2, span(PIECE, c), :], relay.at[span(0, c), :], ypeer) for c in chunks]
+    far_sx = [remote(part.at[3, span(0, c), :], from_x.at[span(PIECE, c), :], xpeer) for c in chunks]
+    far_sy = [remote(part.at[3, span(PIECE, c), :], from_y.at[span(0, c), :], ypeer) for c in chunks]
+
+    near_x.start()
+    near_y.start()
+    own_mate.start()
+    xg[pl.ds(0, ROWS), :] = xn_ref[...]
+    own_mate.wait_recv()
+
+    def add_pair(g, after=None):
+        @pl.loop(0, ROWS // 8)
+        def _(r):
+            rows = pl.ds(pl.multiple_of(r * 8, 8), 8)
+            part[g, rows, :] += mate_in[g, rows, :]
+
+    def hook(g, where, action):
+        return (g, where, action)
+
+    def gather_near():
+        near_x.wait_recv()
+        diag_y.start()
+        near_y.wait_recv()
+        diag_x.start()
+        far_x.start()
+        far_y.start()
+        near_mate.start()
+
+    def gather_diag():
+        diag_y.wait_recv()
+        diag_x.wait_recv()
+        diag_mate.start()
+
+    def gather_far():
+        far_x.wait_recv()
+        far_y.wait_recv()
+        far_mate.start()
+
+    def sum_own():
+        pair_sum[0].wait_recv()
+        add_pair(0)
+
+    def send_near():
+        pair_sum[1].wait_recv()
+        add_pair(1)
+        for c in chunks:
+            near_sx[c].start()
+            near_sy[c].start()
+
+    def send_diag():
+        pair_sum[2].wait_recv()
+        add_pair(2)
+        for c in chunks:
+            diag_sx[c].start()
+            diag_sy[c].start()
+
+    before_h = {
+        (1, 0): near_mate.wait_recv,
+        (1, h_steps // 2): sum_own,
+        (2, 0): diag_mate.wait_recv,
+        (2, h_steps // 2): send_near,
+        (3, 0): far_mate.wait_recv,
+        (3, h_steps // 2): send_diag,
+    }
+    before_n = {
+        (0, 0): gather_near,
+        (1, 0): gather_diag,
+        (2, 0): gather_far,
+        (2, 1): pair_sum[0].wait_send,
+        (3, 0): pair_sum[1].wait_send,
+    }
+    before_n[(2, 0)] = lambda: (gather_far(), pair_sum[0].wait_send())
+    del before_n[(2, 1)]
+
+    def run_hooks(table, g, step):
+        for (hg, hs), action in table.items():
+            @pl.when(jnp.logical_and(g == hg, step == hs))
+            def _():
+                action()
+
+    @pl.loop(0, groups)
+    def _(g):
+        rows = pl.ds(pl.multiple_of(g * (2 * ROWS), 2 * ROWS), 2 * ROWS)
+
+        @pl.loop(0, h_steps)
+        def _(j):
+            run_hooks(before_h, g, j)
+            step = g * h_steps + j
+            slot = lax.rem(step, gu_slots)
+            for copy in gate_copy(step):
+                copy.wait()
+            gate_act = jnp.dot(xg[rows, :], wg_buf[slot], preferred_element_type=jnp.float32)
+            up_act = jnp.dot(xg[rows, :], wu_buf[slot], preferred_element_type=jnp.float32)
+            cols = pl.ds(pl.multiple_of(j * h_tile, h_tile), h_tile)
+            hid[:, cols] = (jax.nn.gelu(gate_act, approximate=True) * up_act).astype(jnp.bfloat16)
+
+            @pl.when(step + gu_slots < groups * h_steps)
+            def _():
+                for copy in gate_copy(step + gu_slots):
+                    copy.start()
+
+        @pl.loop(0, n_steps)
+        def _(n):
+            run_hooks(before_n, g, n)
+            step = g * n_steps + n
+            slot = lax.rem(step, d_slots)
+            down_copy(step).wait()
+            res = jnp.dot(hid[...], wd_buf[slot], preferred_element_type=jnp.float32)
+            cols = pl.ds(pl.multiple_of(n * n_tile, n_tile), n_tile)
+            part[g, :, cols] = res[:ROWS]
+            mate_out[lax.rem(g, 2), :, cols] = res[ROWS:]
+
+            @pl.when(step + d_slots < groups * n_steps)
+            def _():
+                down_copy(step + d_slots).start()
+
+        for hg in range(groups):
+            @pl.when(g == hg)
+            def _():
+                pair_sum[hg].start()
+
+    pair_sum[3].wait_recv()
+    add_pair(3)
+    for c in chunks:
+        diag_sy[c].wait_recv()
+        part[3, pl.ds(c * SUB, SUB), :] += relay[pl.ds(c * SUB, SUB), :]
+        far_sx[c].start()
+        diag_sx[c].wait_recv()
+        part[3, pl.ds(PIECE + c * SUB, SUB), :] += relay[pl.ds(PIECE + c * SUB, SUB), :]
+        far_sy[c].start()
+    for c in chunks:
+        near_sx[c].wait_recv()
+        near_sy[c].wait_recv()
+    part[0] = part[0] + xmid_ref[...]
+    part[0, pl.ds(0, PIECE), :] += from_x[pl.ds(0, PIECE), :]
+    part[0, pl.ds(PIECE, PIECE), :] += from_y[pl.ds(PIECE, PIECE), :]
+    for c in chunks:
+        low, high = pl.ds(c * SUB, SUB), pl.ds(PIECE + c * SUB, SUB)
+        far_sx[c].wait_recv()
+        out_ref[high, :] = (part[0, high, :] + from_x[high, :]).astype(out_ref.dtype)
+        far_sy[c].wait_recv()
+        out_ref[low, :] = (part[0, low, :] + from_y[low, :]).astype(out_ref.dtype)
+    for copy in ([own_mate, near_x, near_y, diag_y, diag_x, far_x, far_y, near_mate, diag_mate, far_mate]
+                 + pair_sum[2:] + near_sx + near_sy + diag_sx + diag_sy + far_sx + far_sy):
+        copy.wait_send()
+
+
+def exchange_mlp(num_tp, xn_mid, x_mid, w_gate, w_up, w_down):
+    width = xn_mid.shape[1]
+    hidden = w_gate.shape[1]
+    h_tile, n_tile = 256, 512
+    gu_slots, d_slots = 3, 3
+    groups = num_tp // 2
+    copies = 10 + groups + 6 * (PIECE // SUB)
+    f32, bf16 = jnp.float32, jnp.bfloat16
+    vmem = pl.BlockSpec(memory_space=pltpu.VMEM)
+    hbm = pl.BlockSpec(memory_space=pl.ANY)
+    return pl.pallas_call(
+        functools.partial(mlp_kernel, num_tp),
+        out_shape=jax.ShapeDtypeStruct((ROWS, width), bf16),
+        in_specs=[vmem, vmem, hbm, hbm, hbm],
+        out_specs=vmem,
+        scratch_shapes=[
+            pltpu.VMEM((num_tp * ROWS, width), bf16),
+            pltpu.VMEM((2 * ROWS, hidden), bf16),
+            pltpu.VMEM((gu_slots, width, h_tile), bf16),
+            pltpu.VMEM((gu_slots, width, h_tile), bf16),
+            pltpu.VMEM((d_slots, hidden, n_tile), bf16),
+            pltpu.VMEM((groups, ROWS, width), f32),
+            pltpu.VMEM((2, ROWS, width), f32),
+            pltpu.VMEM((groups, ROWS, width), f32),
+            pltpu.VMEM((ROWS, width), f32),
+            pltpu.VMEM((ROWS, width), f32),
+            pltpu.VMEM((ROWS, width), f32),
+            pltpu.SemaphoreType.DMA((gu_slots,)),
+            pltpu.SemaphoreType.DMA((gu_slots,)),
+            pltpu.SemaphoreType.DMA((d_slots,)),
+            pltpu.SemaphoreType.DMA((copies,)),
+            pltpu.SemaphoreType.DMA((copies,)),
+        ],
+        compiler_params=pltpu.CompilerParams(
+            collective_id=0, has_side_effects=True, vmem_limit_bytes=67043328),
+        cost_estimate=pl.CostEstimate(flops=6 * num_tp * ROWS * width * hidden,
+                                      bytes_accessed=6 * width * hidden * groups, transcendentals=0),
+        name='exchange_mlp',
+    )(xn_mid, x_mid, w_gate, w_up, w_down)
 
 
 def rms_scale(values, gain_vec):
@@ -65,13 +331,8 @@
     def per_device(hidden_in, k_cache, v_cache, cache_len, norm_attn, norm_mlp, w_q, w_k, w_v, w_o, w_gate, w_up, w_down):
         x_mid, k_new, v_new = attention_block(hidden_in, k_cache, v_cache, cache_len, norm_attn, w_q, w_k, w_v, w_o)
         xn_mid = rms_scale(x_mid, norm_mlp)
-        group_rows = lax.all_gather(xn_mid, 'tp', axis=0, tiled=True)
-        gate_act = jnp.dot(group_rows, w_gate, preferred_element_type=jnp.float32)
-        up_act = jnp.dot(group_rows, w_up, preferred_element_type=jnp.float32)
-        hidden_act = (jax.nn.gelu(gate_act, approximate=True) * up_act).astype(jnp.bfloat16)
-        part_sum = jnp.dot(hidden_act, w_down, preferred_element_type=jnp.float32)
-        down_sum = lax.psum_scatter(part_sum, 'tp', scatter_dimension=0, tiled=True)
-        return (x_mid + down_sum).astype(jnp.bfloat16), k_new, v_new
+        hidden_out = exchange_mlp(mesh.shape['tp'], xn_mid, x_mid, w_gate, w_up, w_down)
+        return hidden_out, k_new, v_new
 
     return jax.shard_map(
         per_device,

time: 326 us -> 198 us (0.61)
  waiting for transfers between devices: 162 us -> 0 us
  Pallas kernels: 0 us -> 119 us
  matrix products: 133 us -> 61.9 us
  between operations: 14.2 us -> 0.88 us
  other arithmetic: 14.2 us -> 7.38 us
  local copies, waits for them, and re-layouts: 2.48 us -> 8.03 us
    pallas_call x0 -> x1, Pallas kernels: none -> 119 us  [exchange_mlp(): pl.pallas_call(functools.partial(mlp_kernel, num_tp), out_shape=jax.Shape...]
    reduce_scatter x1 -> x0, waiting for transfers between devices: 108 us -> none  [per_device(): down_sum = lax.psum_scatter(part_sum, 'tp', scatter_dimension=0, tiled=True)]
    dot_general x3 -> x0, matrix products: 69.6 us -> none  [the longest x1 24.1 us: per_device(): gate_act = jnp.dot(group_rows, w_gate, preferred_element_type=jnp.float32)]
    all_gather x1 -> x0, waiting for transfers between devices: 53.1 us -> none  [per_device(): group_rows = lax.all_gather(xn_mid, 'tp', axis=0, tiled=True)]
    unnamed x28 -> x27, local copies, waits for them, and re-layouts: 2.48 us -> 8.03 us
    convert_element_type x1 -> x0, other arithmetic: 3.41 us -> none  [per_device(): return ((x_mid + down_sum).astype(jnp.bfloat16), k_new, v_new)]
  transfers between devices with their start and end apart: 2 -> 0, of which waited for: 2 -> 0; matrix products, arithmetic and copies ran while one was open for 0% -> 0% of each run, Pallas kernels for 0% -> 0%
where the time goes in v1:
time: 198 us; the launch traced here: 197 us
  Pallas kernels  119 us (60%)
  matrix products  61.9 us (31%)
  local copies, waits for them, and re-layouts  8.03 us (4%)
  other arithmetic  7.38 us (4%)
    pallas_call x1, Pallas kernels, exchange_mlp(): pl.pallas_call(functools.partial(mlp_kernel, num_tp), out_shape=jax.Shape...  119 us
    dot_general x1, matrix products, attend(): jnp.einsum('bht,btd->bhd', hist_prob, v_cache, preferred_element_type=jnp...  16.7 us
    dot_general x1, matrix products, attend(): jnp.einsum('bhd,btd->bht', q_rot, k_cache, preferred_element_type=jnp.flo...  15 us
    dot_general x1, matrix products, attention_block(): jnp.dot(attn_out.reshape(num_rows, num_heads * head_dim), w_o, preferred_...  13.1 us
    dot_general x1, matrix products, attention_block(): jnp.dot(normed, w_q, preferred_element_type=jnp.float32)  13 us
    unnamed x27, local copies, waits for them, and re-layouts  8.03 us

profile of v1, /device:TPU:0, one launch (start us, length us, event | category | flops | bytes accessed | tf_op | source)
XLA Modules:
  0.0 197.1 jit_solution(4972806475642096925)
XLA Ops:
  0.6 0.7 convert_add_fusion.1
  1.3 1.5 fusion.2
  2.9 0.0 copy-start.1
  2.9 2.5 %fusion.23 = f32[128,256]{1,0:T(8,128)S(1)} fusion(bf16[4096,256]{1,0:T(8,128)(2,1)} %param.20, bf16[128,4096]{1,0:T(8,128)(2,1)} %param.13, f32[4096]{0:T(1024)S(1)} %convert_add_fusion.1, f32[128]{0:T(128)S(1)} %add_rsqrt_fusion.1), kind=kOutput, calls=%fused_computation.46 | convolution fusion | flops 270532608 | bytes 3293696 | tf_op jit(solution)/shard_map/dot_general | solution.py:315
  5.4 0.3 subtract_convert_fusion
  5.8 13.0 %fusion.25 = f32[128,4096]{1,0:T(8,128)S(1)} fusion(bf16[4096,4096]{1,0:T(8,128)(2,1)} %param.19, bf16[128,4096]{1,0:T(8,128)(2,1)S(1)} %copy-done.1, f32[4096]{0:T(1024)S(1)} %convert_add_fusion.1, f32[128]{0:T(128)S(1)} %add_rsqrt_fusion.1), kind=kOutput, calls=%fused_computation.47 | convolution fusion | flops 4297064448 | bytes 36717056 | tf_op jit(solution)/shard_map/dot_general | solution.py:314
  18.8 0.7 copy.18
  19.5 0.3 multiply_subtract_fusion
  19.7 0.0 copy-start.6
  19.8 0.0 copy-done.7
  19.8 0.0 copy-done.8
  19.8 0.4 fusion.10
  20.2 0.5 copy-done.5
  20.7 0.3 copy-done.6
  21.1 0.1 iota_compare_fusion
  21.2 15.0 %select_reduce_fusion = (f32[128,16]{1,0:T(8,128)S(1)}, f32[128,16,512]{2,1,0:T(8,128)S(1)}) fusion(pred[128,512]{1,0:T(8,128)(4,1)S(1)} %iota_compare_fusion, bf16[128,512,256]{2,1,0:T(8,128)(2,1)} %param.14, f32[128,16,128]{2,1,0:T(8,128)} %copy-done.6, f32[128,16,128]{2,1,0:T(8,128)} %copy-done.5), kind=kOutput, calls=%fused_computation.3 | convolution fusion | flops 540538880 | bytes 39919616 | tf_op jit(solution)/shard_map/bhd,btd->bht/dot_general | solution.py:294
  36.2 0.0 copy-start.2
  36.2 0.0 copy-start.11
  36.3 1.7 fusion
  38.0 0.4 copy-done
  38.4 1.3 copy-done.11
  39.6 1.1 fusion.27
  40.8 16.7 %add_convert_fusion = bf16[128,16,256]{2,1,0:T(8,128)(2,1)S(1)} fusion(bf16[128,512,256]{2,1,0:T(8,128)(2,1)} %param.15, f32[128,16,512]{2,1,0:T(8,128)} %copy-done, f32[128,16]{1,0:T(8,128)S(1)} %get-tuple-element.6, f32[128,16]{1,0:T(8,128)S(1)} %max.3, pred[128,512]{1,0:T(8,128)(4,1)S(1)} %iota_compare_fusion, f32[128,256]{1,0:T(8,128)S(1)} %get-tuple-element.13, ...), kind=kOutput, calls=%fused_computation.15 | convolution fusion | flops 542638080 | bytes 39018496 | tf_op jit(solution)/shard_map/bht,btd->bhd/dot_general | solution.py:304
  57.5 0.4 copy.19
  57.9 0.8 copy-done.3
  58.7 13.1 %multiply_reduce_fusion = (f32[128]{0:T(128)S(1)}, f32[128,4096]{1,0:T(8,128)S(1)}) fusion(bf16[128,4096]{1,0:T(8,128)(2,1)S(1)} %bitcast.18, bf16[4096,4096]{1,0:T(8,128)(2,1)} %param.22, bf16[128,4096]{1,0:T(8,128)(2,1)S(1)} %copy-done.3), kind=kOutput, calls=%fused_computation.14 | convolution fusion | flops 4297064448 | bytes 37749248 | tf_op jit(solution)/shard_map/dot_general | solution.py:321
  71.9 0.0 copy-done.9
  71.9 1.3 copy-done.4
  73.2 1.2 multiply_convert_fusion.xn_ref
  74.4 118.9 %exchange_mlp.1 = bf16[128,4096]{1,0:T(8,128)(2,1)} custom-call(bf16[128,4096]{1,0:T(8,128)(2,1)} %multiply_convert_fusion.xn_ref, f32[128,4096]{1,0:T(8,128)} %copy-done.4, bf16[4096,2048]{1,0:T(8,128)(2,1)} %wg_hbm.1, bf16[4096,2048]{1,0:T(8,128)(2,1)} %wu_hbm.1, bf16[2048,4096]{1,0:T(8,128)(2,1)} %wd_hbm.1), custom_call_target="tpu_custom_call" | custom-call | flops 51539607552 | bytes 201326592 | tf_op jit(solution)/shard_map/exchange_mlp/pallas_call | solution.py:242
  193.4 1.4 pad_maximum_fusion
  194.8 2.3 %copy.23 = bf16[128,4096]{1,0:T(8,128)(2,1)} copy(bf16[128,4096]{1,0:T(8,128)(2,1)} %exchange_mlp.1) | data formatting | bytes 2097152
  (19 shorter events, 0.1 us)
Async XLA Ops:
  2.8 2.5 %copy-start.10 = (s32[128]{0:T(128)S(1)}, s32[128]{0:T(128)}, u32[]{:S(2)}) copy-start(s32[128]{0:T(128)} %param.16) | copy-start | bytes 1540
  2.9 2.9 %copy-start.1 = (bf16[128,4096]{1,0:T(8,128)(2,1)S(1)}, bf16[128,4096]{1,0:T(8,128)(2,1)}, u32[]{:S(2)}) copy-start(bf16[128,4096]{1,0:T(8,128)(2,1)} %param.13) | copy-start | bytes 3145732
  5.7 14.0 %copy-start.7 = (bf16[128,128]{1,0:T(8,128)(2,1)}, bf16[128,128]{1,0:T(8,128)(2,1)S(1)}, u32[]{:S(2)}) copy-start(bf16[128,128]{1,0:T(8,128)(2,1)S(1)} %get-tuple-element.7) | copy-start | bytes 98308
  5.7 14.0 %copy-start.8 = (bf16[128,128]{1,0:T(8,128)(2,1)}, bf16[128,128]{1,0:T(8,128)(2,1)S(1)}, u32[]{:S(2)}) copy-start(bf16[128,128]{1,0:T(8,128)(2,1)S(1)} %get-tuple-element.8) | copy-start | bytes 98308
  19.7 1.0 copy-start.5
  19.7 1.3 copy-start.6
  36.2 2.1 %copy-start = (f32[128,16,512]{2,1,0:T(8,128)}, f32[128,16,512]{2,1,0:T(8,128)S(1)}, u32[]{:S(2)}) copy-start(f32[128,16,512]{2,1,0:T(8,128)S(1)} %get-tuple-element.12) | copy-start | bytes 12582916
  36.2 2.1 %copy-start.2 = (bf16[128,4096]{1,0:T(8,128)(2,1)S(1)}, bf16[128,4096]{1,0:T(8,128)(2,1)}, u32[]{:S(2)}) copy-start(bf16[128,4096]{1,0:T(8,128)(2,1)} %param.13) | copy-start | bytes 3145732
  36.2 3.4 %copy-start.11 = (bf16[4096,256]{1,0:T(8,128)(2,1)S(1)}, bf16[4096,256]{1,0:T(8,128)(2,1)}, u32[]{:S(2)}) copy-start(bf16[4096,256]{1,0:T(8,128)(2,1)} %param.21) | copy-start | bytes 6291460
  57.5 1.2 copy-start.3
  58.7 13.2 %copy-start.9 = (bf16[4096]{0:T(1024)(128)(2,1)S(1)}, bf16[4096]{0:T(1024)(128)(2,1)}, u32[]{:S(2)}) copy-start(bf16[4096]{0:T(1024)(128)(2,1)} %param.18) | copy-start | bytes 24580
  71.8 1.4 copy-start.4

commit v2 on v1

v2 whole, which is shorter than its diff:
```python
import functools

import jax
import jax.numpy as jnp
from jax import lax
from jax.experimental import pallas as pl
from jax.experimental.pallas import tpu as pltpu
from jax.sharding import PartitionSpec as P

ROWS = 128
PIECE = 64
SUB = 32


def mlp_kernel(num_tp, xn_ref, xmid_ref, wg_hbm, wu_hbm, wd_hbm, out_ref,
               xg, hid, wg_buf, wu_buf, wd_buf, part, mate_out, mate_in, relay, from_x, from_y,
               wg_sem, wu_sem, wd_sem, send_sem, recv_sem):
    me = lax.axis_index('tp')
    mate = me + 1 - 2 * lax.rem(me, 2)
    xpeer = me + 2 - 4 * lax.rem(me // 2, 2)
    ypeer = me + 4 - 8 * (me // 4)

    h_tile = wg_buf.shape[2]
    n_tile = wd_buf.shape[2]
    h_steps = hid.shape[2] // h_tile
    n_steps = wd_hbm.shape[1] // n_tile
    groups = num_tp // 2
    gu_slots = wg_buf.shape[0]
    d_slots = wd_buf.shape[0]

    def gate_copy(step):
        cols = pl.ds(pl.multiple_of(lax.rem(step, h_steps) * h_tile, h_tile), h_tile)
        slot = lax.rem(step, gu_slots)
        return (pltpu.make_async_copy(wg_hbm.at[:, cols], wg_buf.at[slot], wg_sem.at[slot]),
                pltpu.make_async_copy(wu_hbm.at[:, cols], wu_buf.at[slot], wu_sem.at[slot]))

    def down_copy(step):
        cols = pl.ds(pl.multiple_of(lax.rem(step, n_steps) * n_tile, n_tile), n_tile)
        slot = lax.rem(step, d_slots)
        return pltpu.make_async_copy(wd_hbm.at[:, cols], wd_buf.at[slot], wd_sem.at[slot])

    for step in range(gu_slots):
        for copy in gate_copy(jnp.int32(step)):
            copy.start()
    for step in range(d_slots):
        down_copy(jnp.int32(step)).start()

    barrier = pltpu.get_barrier_semaphore()
    for peer in (mate, xpeer, ypeer):
        pl.semaphore_signal(barrier, inc=1, device_id={'tp': peer}, device_id_type=pl.DeviceIdType.MESH)
    pl.semaphore_wait(barrier, 3)

    count = [0]

    def remote(src, dst, peer):
        k = count[0]
        count[0] += 1
        return pltpu.make_async_remote_copy(
            src_ref=src, dst_ref=dst, send_sem=send_sem.at[k], recv_sem=recv_sem.at[k],
            device_id={'tp': peer}, device_id_type=pl.DeviceIdType.MESH)

    def rows_of(start, size):
        return xg.at[pl.ds(start, size), :]

    top, bot = xn_ref.at[pl.ds(0, PIECE), :], xn_ref.at[pl.ds(PIECE, PIECE), :]
    chunks = range(PIECE // SUB)

    def span(lead, c):
        return pl.ds(lead + c * SUB, SUB)

    own_mate = remote(xn_ref, rows_of(128, 128), mate)
    near_x = remote(top, rows_of(256, 64), xpeer)
    near_y = remote(bot, rows_of(320, 64), ypeer)
    diag_y = remote(rows_of(256, 64), rows_of(512, 64), ypeer)
    diag_x = remote(rows_of(320, 64), rows_of(576, 64), xpeer)
    far_x = [remote(xn_ref.at[span(PIECE, c), :], xg.at[span(768, c), :], xpeer) for c in chunks]
    far_y = [remote(xn_ref.at[span(0, c), :], xg.at[span(832, c), :], ypeer) for c in chunks]
    near_mate = remote(rows_of(256, 128), rows_of(384, 128), mate)
    diag_mate = remote(rows_of(512, 128), rows_of(640, 128), mate)
    far_mate = remote(rows_of(768, 128), rows_of(896, 128), mate)
    width = xn_ref.shape[1]
    quarters = 4
    side = [pl.ds(i * (width // quarters), width // quarters) for i in range(quarters)]
    pair = [[remote(mate_out.at[(g + 1) % 2, :, cols], mate_in.at[g, :, cols], mate) for cols in side]
            for g in range(groups)]
    near_sx = [remote(part.at[1, span(0, c), :], from_x.at[span(0, c), :], xpeer) for c in chunks]
    near_sy = [remote(part.at[1, span(PIECE, c), :], from_y.at[span(PIECE, c), :], ypeer) for c in chunks]
    diag_sx = [remote(part.at[2, span(0, c), :], relay.at[span(PIECE, c), :], xpeer) for c in chunks]
    diag_sy = [remote(part.at[2, span(PIECE, c), :], relay.at[span(0, c), :], ypeer) for c in chunks]
    far_sx = [remote(part.at[3, span(0, c), :], from_x.at[span(PIECE, c), :], xpeer) for c in chunks]
    far_sy = [remote(part.at[3, span(PIECE, c), :], from_y.at[span(0, c), :], ypeer) for c in chunks]

    near_x.start()
    near_y.start()
    far_x[0].start()
    far_y[0].start()
    own_mate.start()
    xg[pl.ds(0, ROWS), :] = xn_ref[...]
    own_mate.wait_recv()

    def add_pair(g):
        for copy in pair[g]:
            copy.wait_recv()

        @pl.loop(0, ROWS // 8)
        def _(r):
            rows = pl.ds(pl.multiple_of(r * 8, 8), 8)
            part[g, rows, :] += mate_in[g, rows, :]

    def gather_near():
        near_x.wait_recv()
        diag_y.start()
        near_y.wait_recv()
        diag_x.start()
        far_x[1].start()
        far_y[1].start()
        near_mate.start()

    def gather_diag():
        diag_y.wait_recv()
        diag_x.wait_recv()
        diag_mate.start()

    def gather_far():
        for c in chunks:
            far_x[c].wait_recv()
            far_y[c].wait_recv()
        far_mate.start()

    def send_near():
        add_pair(1)
        for c in chunks:
            near_sx[c].start()
            near_sy[c].start()

    def send_diag():
        add_pair(2)
        for c in chunks:
            diag_sx[c].start()
            diag_sy[c].start()

    def free_slot(g):
        for copy in pair[g]:
            copy.wait_send()

    def start_diag():
        send_near()
        gather_diag()
        diag_mate.wait_recv()

    def start_far():
        send_diag()
        far_mate.wait_recv()

    def pass_on(c):
        diag_sy[c].wait_recv()
        part[3, span(0, c), :] += relay[span(0, c), :]
        far_sx[c].start()
        diag_sx[c].wait_recv()
        part[3, span(PIECE, c), :] += relay[span(PIECE, c), :]
        far_sy[c].start()

    before_h = {
        (0, h_steps - 1): gather_near,
        (1, 0): near_mate.wait_recv,
        (2, 0): start_diag,
        (2, h_steps - 1): gather_far,
        (3, 0): start_far,
    }
    before_n = {
        (3, 0): lambda: free_slot(1),
        (0, 0): lambda: free_slot(2),
        (0, n_steps // 2): lambda: add_pair(3),
        (0, n_steps - 2): lambda: pass_on(0),
    }

    def run_hooks(table, g, step):
        for (hg, hs), action in table.items():
            @pl.when(jnp.logical_and(g == hg, step == hs))
            def _():
                action()

    @pl.loop(0, groups + 1)
    def _(turn):
        @pl.when(turn < groups)
        def _():
            rows = pl.ds(pl.multiple_of(turn * (2 * ROWS), 2 * ROWS), 2 * ROWS)
            keep = jnp.minimum(turn, 1)

            @pl.loop(0, h_steps)
            def _(j):
                run_hooks(before_h, turn, j)
                step = turn * h_steps + j
                slot = lax.rem(step, gu_slots)
                for copy in gate_copy(step):
                    copy.wait()
                gate_act = jnp.dot(xg[rows, :], wg_buf[slot], preferred_element_type=jnp.float32)
                up_act = jnp.dot(xg[rows, :], wu_buf[slot], preferred_element_type=jnp.float32)
                cols = pl.ds(pl.multiple_of(j * h_tile, h_tile), h_tile)
                hid[keep, :, cols] = (jax.nn.gelu(gate_act, approximate=True) * up_act).astype(jnp.bfloat16)

                @pl.when(step + gu_slots < groups * h_steps)
                def _():
                    for copy in gate_copy(step + gu_slots):
                        copy.start()

        @pl.when(turn > 0)
        def _():
            g = lax.rem(turn, groups)
            keep = jnp.minimum(g, 1)

            @pl.loop(0, n_steps)
            def _(n):
                run_hooks(before_n, g, n)
                step = (turn - 1) * n_steps + n
                slot = lax.rem(step, d_slots)
                down_copy(step).wait()
                res = jnp.dot(hid[keep], wd_buf[slot], preferred_element_type=jnp.float32)
                cols = pl.ds(pl.multiple_of(n * n_tile, n_tile), n_tile)
                part[g, :, cols] = res[:ROWS]
                mate_out[lax.rem(g + 1, 2), :, cols] = res[ROWS:]

                for hg in range(groups):
                    for i in range(quarters):
                        @pl.when(jnp.logical_and(g == hg, n == (i + 1) * n_steps // quarters - 1))
                        def _():
                            pair[hg][i].start()

                @pl.when(step + d_slots < groups * n_steps)
                def _():
                    down_copy(step + d_slots).start()


    add_pair(0)
    for c in chunks:
        near_sx[c].wait_recv()
        near_sy[c].wait_recv()
    part[0] = part[0] + xmid_ref[...]
    part[0, pl.ds(0, PIECE), :] += from_x[pl.ds(0, PIECE), :]
    part[0, pl.ds(PIECE, PIECE), :] += from_y[pl.ds(PIECE, PIECE), :]
    for c in chunks[1:]:
        pass_on(c)
    for c in chunks:
        low, high = span(0, c), span(PIECE, c)
        far_sx[c].wait_recv()
        out_ref[high, :] = (part[0, high, :] + from_x[high, :]).astype(out_ref.dtype)
        far_sy[c].wait_recv()
        out_ref[low, :] = (part[0, low, :] + from_y[low, :]).astype(out_ref.dtype)
    for copy in ([own_mate, near_x, near_y, diag_y, diag_x, near_mate, diag_mate, far_mate]
                 + far_x + far_y + pair[3] + pair[0]
                 + near_sx + near_sy + diag_sx + diag_sy + far_sx + far_sy):
        copy.wait_send()


def exchange_mlp(num_tp, xn_mid, x_mid, w_gate, w_up, w_down):
    width = xn_mid.shape[1]
    hidden = w_gate.shape[1]
    h_tile, n_tile = 256, 512
    gu_slots, d_slots = 3, 3
    groups = num_tp // 2
    copies = 8 + 4 * groups + 8 * (PIECE // SUB)
    f32, bf16 = jnp.float32, jnp.bfloat16
    vmem = pl.BlockSpec(memory_space=pltpu.VMEM)
    hbm = pl.BlockSpec(memory_space=pl.ANY)
    return pl.pallas_call(
        functools.partial(mlp_kernel, num_tp),
        out_shape=jax.ShapeDtypeStruct((ROWS, width), bf16),
        in_specs=[vmem, vmem, hbm, hbm, hbm],
        out_specs=vmem,
        scratch_shapes=[
            pltpu.VMEM((num_tp * ROWS, width), bf16),
            pltpu.VMEM((2, 2 * ROWS, hidden), bf16),
            pltpu.VMEM((gu_slots, width, h_tile), bf16),
            pltpu.VMEM((gu_slots, width, h_tile), bf16),
            pltpu.VMEM((d_slots, hidden, n_tile), bf16),
            pltpu.VMEM((groups, ROWS, width), f32),
            pltpu.VMEM((2, ROWS, width), f32),
            pltpu.VMEM((groups, ROWS, width), f32),
            pltpu.VMEM((ROWS, width), f32),
            pltpu.VMEM((ROWS, width), f32),
            pltpu.VMEM((ROWS, width), f32),
            pltpu.SemaphoreType.DMA((gu_slots,)),
            pltpu.SemaphoreType.DMA((gu_slots,)),
            pltpu.SemaphoreType.DMA((d_slots,)),
            pltpu.SemaphoreType.DMA((copies,)),
            pltpu.SemaphoreType.DMA((copies,)),
        ],
        compiler_params=pltpu.CompilerParams(
            collective_id=0, has_side_effects=True, vmem_limit_bytes=67043328),
        cost_estimate=pl.CostEstimate(flops=6 * num_tp * ROWS * width * hidden,
                                      bytes_accessed=6 * width * hidden * groups, transcendentals=0),
        name='exchange_mlp',
    )(xn_mid, x_mid, w_gate, w_up, w_down)


def rope_tables(positions, head_dim):
    half_dim = head_dim // 2
    inv_freq = 10000.0 ** (-2.0 * jnp.arange(half_dim, dtype=jnp.float32) / head_dim)
    angles = positions.astype(jnp.float32)[:, None] * inv_freq[None, :]
    return jnp.cos(angles), jnp.sin(angles)


TEAM = 8
BLOCK = 128
AHEAD = 4


def attention_kernel(order, lens, hid_ref, ga_ref, gm_ref, cos_ref, sin_ref, wk_hbm, wv_hbm, wq_hbm, wo_hbm,
                     kc_hbm, vc_hbm, xn_out, xmid_out, knew_out, vnew_out,
                     w_buf, k_buf, v_buf, xn, q_lo, q_hi, o_lo, o_hi, k_row, v_row, squares,
                     w_sem, k_sem, v_sem):
    num_rows, width = hid_ref.shape
    head_dim = wk_hbm.shape[1]
    half = head_dim // 2
    heads = wq_hbm.shape[1] // head_dim
    tiles = wo_hbm.shape[1] // head_dim
    teams = num_rows // TEAM
    slots = k_buf.shape[0]
    w_slots = w_buf.shape[0]
    max_units = kc_hbm.shape[1] // BLOCK
    f32, bf16 = jnp.float32, jnp.bfloat16

    def tile_copy(src, tile, slot):
        cols = pl.ds(pl.multiple_of(tile * head_dim, head_dim), head_dim)
        return pltpu.make_async_copy(src.at[:, cols], w_buf.at[slot], w_sem.at[slot])

    def head_copy(head):
        return tile_copy(wq_hbm, head, lax.rem(head + 2, w_slots))

    def out_copy(tile):
        return tile_copy(wo_hbm, tile, tile)

    def units_of(team):
        longest = lens[order[team * TEAM + TEAM - 1]]
        return jnp.maximum((longest + BLOCK - 1) // BLOCK, 1)

    def key_copy(team, r, n):
        slot, span = lax.rem(team, slots), pl.ds(0, n * BLOCK)
        return pltpu.make_async_copy(kc_hbm.at[order[team * TEAM + r], span, :],
                                     k_buf.at[slot, r, span, :], k_sem.at[slot, r])

    def value_copy(team, r, n):
        slot, span = lax.rem(team, slots), pl.ds(0, n * BLOCK)
        return pltpu.make_async_copy(vc_hbm.at[order[team * TEAM + r], span, :],
                                     v_buf.at[slot, r, span, :], v_sem.at[slot, r])

    def fetch(team):
        units = units_of(team)
        for n in range(1, max_units + 1):
            @pl.when(units == n)
            def _():
                for r in range(TEAM):
                    key_copy(team, r, n).start()
                    value_copy(team, r, n).start()

    def normalise(src, gain_ref, dst):
        gain = 1.0 + gain_ref[...].astype(f32)[None, :]

        @pl.loop(0, num_rows // 16)
        def _(i):
            rows = pl.ds(pl.multiple_of(i * 16, 16), 16)
            wide = src[rows, :].astype(f32)
            inv = lax.rsqrt(jnp.mean(wide * wide, axis=-1, keepdims=True) + 1e-6)
            dst[rows, :] = (wide * inv * gain).astype(bf16)

    first = [tile_copy(wk_hbm, 0, 0), tile_copy(wv_hbm, 0, 1)]
    for copy in first:
        copy.start()
    for head in range(AHEAD - 2):
        head_copy(jnp.int32(head)).start()
    normalise(hid_ref, ga_ref, xn)

    def rotate(lin):
        low, high = lin[:, :half], lin[:, half:]
        cos_t, sin_t = cos_ref[...], sin_ref[...]
        return low * cos_t - high * sin_t, high * cos_t + low * sin_t

    first[0].wait()
    head_copy(jnp.int32(AHEAD - 2)).start()
    low, high = rotate(jnp.dot(xn[...], w_buf[0], preferred_element_type=f32))
    key = jnp.concatenate([low, high], axis=-1).astype(bf16)
    knew_out[...] = key
    k_row[...] = key.astype(f32)
    first[1].wait()
    head_copy(jnp.int32(AHEAD - 1)).start()
    value = jnp.dot(xn[...], w_buf[1], preferred_element_type=f32).astype(bf16)
    vnew_out[...] = value
    v_row[...] = value.astype(f32)

    early = range(slots - 1)

    @pl.loop(0, heads)
    def _(head):
        head_copy(head).wait()

        @pl.when(head + AHEAD < heads)
        def _():
            head_copy(head + AHEAD).start()
        for team in early:
            @pl.when(head == heads - AHEAD + team)
            def _():
                fetch(jnp.int32(team))
        low, high = rotate(jnp.dot(xn[...], w_buf[lax.rem(head + 2, w_slots)], preferred_element_type=f32))
        spots = pl.ds(head, num_rows, stride=heads)
        q_lo[spots, :] = (low * head_dim ** -0.5).astype(bf16).astype(f32)
        q_hi[spots, :] = (high * head_dim ** -0.5).astype(bf16).astype(f32)

    def attend(team, n):
        slot = lax.rem(team, slots)
        size = n * BLOCK
        rows = [order[team * TEAM + r] for r in range(TEAM)]
        spans = [pl.ds(pl.multiple_of(row * heads, heads), heads) for row in rows]
        for r in range(TEAM):
            key_copy(team, r, n).wait()
        wide = [jnp.concatenate([q_lo[span, :], q_hi[span, :]], axis=-1) for span in spans]
        scores = [lax.dot_general(wide[r].astype(bf16), k_buf[slot, r, pl.ds(0, size), :], (((1,), (1,)), ((), ())),
                                  preferred_element_type=f32) for r in range(TEAM)]
        for r in range(TEAM):
            value_copy(team, r, n).wait()
        place = lax.broadcasted_iota(jnp.int32, scores[0].shape, 1)
        probs, news = [], []
        for r in range(TEAM):
            score = jnp.where(place < lens[rows[r]], scores[r], -jnp.inf)
            fresh = jnp.sum(wide[r] * k_row[pl.ds(rows[r], 1), :], axis=-1, keepdims=True)
            peak = jnp.maximum(jnp.max(score, axis=-1, keepdims=True), fresh)
            weight = jnp.exp(score - peak)
            fresh = jnp.exp(fresh - peak)
            scale = 1.0 / (jnp.sum(weight, axis=-1, keepdims=True) + fresh)
            probs.append((weight * scale).astype(bf16))
            news.append((fresh * scale).astype(bf16).astype(f32))
        for r in range(TEAM):
            mixed = jnp.dot(probs[r], v_buf[slot, r, pl.ds(0, size), :], preferred_element_type=f32)
            mixed = mixed + news[r] * v_row[pl.ds(rows[r], 1), :]
            mixed = mixed.astype(bf16).astype(f32)
            o_lo[spans[r], :] = mixed[:, :half]
            o_hi[spans[r], :] = mixed[:, half:]

    share = tiles // teams

    @pl.loop(0, teams)
    def _(team):
        @pl.when(team + slots - 1 < teams)
        def _():
            fetch(team + slots - 1)
        for part in range(share):
            out_copy(team * share + part).start()
        units = units_of(team)
        for n in range(1, max_units + 1):
            @pl.when(units == n)
            def _():
                attend(team, n)

    for head in range(heads):
        spots = pl.ds(head, num_rows, stride=heads)
        xn[:, pl.ds(head * head_dim, half)] = o_lo[spots, :].astype(bf16)
        xn[:, pl.ds(head * head_dim + half, half)] = o_hi[spots, :].astype(bf16)
    squares[...] = jnp.zeros_like(squares)

    @pl.loop(0, tiles)
    def _(tile):
        out_copy(tile).wait()
        cols = pl.ds(pl.multiple_of(tile * head_dim, head_dim), head_dim)
        mixed = hid_ref[:, cols].astype(f32) + jnp.dot(xn[...], w_buf[tile], preferred_element_type=f32)
        xmid_out[:, cols] = mixed
        mixed = mixed * mixed
        squares[...] += mixed[:, :half] + mixed[:, half:]

    gain = 1.0 + gm_ref[...].astype(f32)[None, :]

    @pl.loop(0, num_rows // 16)
    def _(i):
        rows = pl.ds(pl.multiple_of(i * 16, 16), 16)
        inv = lax.rsqrt(jnp.sum(squares[rows, :], axis=-1, keepdims=True) * (1.0 / width) + 1e-6)
        xn_out[rows, :] = (xmid_out[rows, :] * inv * gain).astype(bf16)


def attention_block(hidden_in, k_cache, v_cache, cache_len, norm_attn, norm_mlp, w_q, w_k, w_v, w_o):
    num_rows, width = hidden_in.shape
    head_dim = w_k.shape[1]
    half = head_dim // 2
    heads = w_q.shape[1] // head_dim
    cos_t, sin_t = rope_tables(cache_len, head_dim)
    spot = jnp.arange(num_rows, dtype=jnp.int32)
    ahead = (cache_len[None, :] < cache_len[:, None]) | (
        (cache_len[None, :] == cache_len[:, None]) & (spot[None, :] < spot[:, None]))
    rank = jnp.sum(ahead.astype(jnp.int32), axis=1)
    order = jnp.sum(jnp.where(rank[:, None] == spot[None, :], spot[:, None], 0), axis=0)
    slots, w_slots = 3, w_o.shape[1] // head_dim
    f32, bf16 = jnp.float32, jnp.bfloat16
    vmem = pl.BlockSpec(memory_space=pltpu.VMEM)
    smem = pl.BlockSpec(memory_space=pltpu.SMEM)
    hbm = pl.BlockSpec(memory_space=pl.ANY)
    team_shape = (slots, TEAM, k_cache.shape[1], head_dim)
    return pl.pallas_call(
        attention_kernel,
        out_shape=[jax.ShapeDtypeStruct((num_rows, width), bf16), jax.ShapeDtypeStruct((num_rows, width), f32),
                   jax.ShapeDtypeStruct((num_rows, head_dim), bf16), jax.ShapeDtypeStruct((num_rows, head_dim), bf16)],
        in_specs=[smem, smem, vmem, vmem, vmem, vmem, vmem, hbm, hbm, hbm, hbm, hbm, hbm],
        out_specs=[vmem] * 4,
        scratch_shapes=[
            pltpu.VMEM((w_slots, width, head_dim), bf16),
            pltpu.VMEM(team_shape, bf16),
            pltpu.VMEM(team_shape, bf16),
            pltpu.VMEM((num_rows, width), bf16),
            pltpu.VMEM((num_rows * heads, half), f32),
            pltpu.VMEM((num_rows * heads, half), f32),
            pltpu.VMEM((num_rows * heads, half), f32),
            pltpu.VMEM((num_rows * heads, half), f32),
            pltpu.VMEM((num_rows, head_dim), f32),
            pltpu.VMEM((num_rows, head_dim), f32),
            pltpu.VMEM((num_rows, half), f32),
            pltpu.SemaphoreType.DMA((w_slots,)),
            pltpu.SemaphoreType.DMA((slots, TEAM)),
            pltpu.SemaphoreType.DMA((slots, TEAM)),
        ],
        compiler_params=pltpu.CompilerParams(vmem_limit_bytes=67043328),
        cost_estimate=pl.CostEstimate(flops=4 * num_rows * width * width, bytes_accessed=4 * width * width,
                                      transcendentals=0),
        name='attention_block',
    )(order, cache_len, hidden_in, norm_attn, norm_mlp, cos_t, sin_t, w_k, w_v, w_q, w_o,
      k_cache, v_cache)


def solution(mesh):
    row_spec = P(('dp', 'tp'), None)
    cache_spec = P(('dp', 'tp'), None, None)
    full_vec = P(None)
    full_mat = P(None, None)

    def per_device(hidden_in, k_cache, v_cache, cache_len, norm_attn, norm_mlp, w_q, w_k, w_v, w_o, w_gate, w_up, w_down):
        xn_mid, x_mid, k_new, v_new = attention_block(
            hidden_in, k_cache, v_cache, cache_len, norm_attn, norm_mlp, w_q, w_k, w_v, w_o)
        hidden_out = exchange_mlp(mesh.shape['tp'], xn_mid, x_mid, w_gate, w_up, w_down)
        return hidden_out, k_new, v_new

    return jax.shard_map(
        per_device,
        mesh=mesh,
        in_specs=(row_spec, cache_spec, cache_spec, P(('dp', 'tp')), full_vec, full_vec,
                  full_mat, full_mat, full_mat, full_mat, P(None, 'tp'), P(None, 'tp'), P('tp', None)),
        out_specs=(row_spec, row_spec, row_spec),
        check_vma=False,
    )
```

time: 198 us -> 166 us (0.84)
  matrix products: 61.9 us -> 0 us
  Pallas kernels: 119 us -> 159 us
  local copies, waits for them, and re-layouts: 8.03 us -> 2.29 us
  other arithmetic: 7.38 us -> 3.22 us
    dot_general x7 -> x0, matrix products: 61.9 us -> none  [the longest x1 16.7 us: attend(): jnp.einsum('bht,btd->bhd', hist_prob, v_cache, preferred_element_type=jnp...]
    pallas_call x0 -> x1, Pallas kernels: none -> 48 us  [attention_block(): pl.pallas_call(attention_kernel, out_shape=[jax.ShapeDtypeStruct((num_row...]
    pallas_call x1, Pallas kernels: 119 us -> 111 us  [exchange_mlp(): pl.pallas_call(functools.partial(mlp_kernel, num_tp), out_shape=jax.Shape...]
    unnamed x27 -> x1, local copies, waits for them, and re-layouts: 8.03 us -> 2.29 us
where the time goes in v2:
time: 166 us; the launch traced here: 165 us
  Pallas kernels  159 us (96%)
  other arithmetic  3.22 us (2%)
  local copies, waits for them, and re-layouts  2.29 us (1%)
    pallas_call x1, Pallas kernels, exchange_mlp(): pl.pallas_call(functools.partial(mlp_kernel, num_tp), out_shape=jax.Shape...  111 us
    pallas_call x1, Pallas kernels, attention_block(): pl.pallas_call(attention_kernel, out_shape=[jax.ShapeDtypeStruct((num_row...  48 us

profile of v2, /device:TPU:0, one launch (start us, length us, event | category | flops | bytes accessed | tf_op | source)
XLA Modules:
  0.0 165.3 jit_solution(8992506823200477556)
XLA Ops:
  0.6 0.9 convert_reduce_fusion
  1.5 0.7 select_reduce_fusion.order
  2.2 0.7 convert_element_type.7
  2.9 1.0 multiply_sine_fusion
  3.9 48.0 %attention_block.1 = (bf16[128,4096]{1,0:T(8,128)(2,1)}, f32[128,4096]{1,0:T(8,128)}, bf16[128,256]{1,0:T(8,128)(2,1)}, bf16[128,256]{1,0:T(8,128)(2,1)}) custom-call(s32[128]{0:T(128)} %select_reduce_fusion.order, s32[128]{0:T(128)} %lens.1, bf16[128,4096]{1,0:T(8,128)(2,1)} %hid_ref.1, bf16[4096]{0:T(1024)(128)(2,1)} %ga_ref.1, bf16[4096]{0:T(1024)(128)(2,1)} %gm_ref.1, ...), custom_call_target="tpu_custom_call" | custom-call | flops 8589934592 | bytes 67108864 | tf_op jit(solution)/shard_map/attention_block/pallas_call | solution.py:494
  51.9 111.1 %exchange_mlp.1 = bf16[128,4096]{1,0:T(8,128)(2,1)} custom-call(bf16[128,4096]{1,0:T(8,128)(2,1)} %get-tuple-element.7.xn_ref, f32[128,4096]{1,0:T(8,128)} %get-tuple-element.8.xmid_ref, bf16[4096,2048]{1,0:T(8,128)(2,1)} %wg_hbm.1, bf16[4096,2048]{1,0:T(8,128)(2,1)} %wu_hbm.1, bf16[2048,4096]{1,0:T(8,128)(2,1)} %wd_hbm.1), custom_call_target="tpu_custom_call" | custom-call | flops 51539607552 | bytes 201326592 | tf_op jit(solution)/shard_map/exchange_mlp/pallas_call | solution.py:265
  163.0 2.3 %copy.17 = bf16[128,4096]{1,0:T(8,128)(2,1)} copy(bf16[128,4096]{1,0:T(8,128)(2,1)} %exchange_mlp.1) | data formatting | bytes 2097152
  (1 shorter events, 0.0 us)

commit v3 on v2

--- a/solution.py
+++ b/solution.py
@@ -5,6 +5,7 @@
 from jax import lax
 from jax.experimental import pallas as pl
 from jax.experimental.pallas import tpu as pltpu
+import numpy as np
 from jax.sharding import PartitionSpec as P
 
 ROWS = 128
@@ -12,9 +13,9 @@
 SUB = 32
 
 
-def mlp_kernel(num_tp, xn_ref, xmid_ref, wg_hbm, wu_hbm, wd_hbm, out_ref,
-               xg, hid, wg_buf, wu_buf, wd_buf, part, mate_out, mate_in, relay, from_x, from_y,
-               wg_sem, wu_sem, wd_sem, send_sem, recv_sem):
+def mlp_kernel(num_tp, xn_ref, xmid_hbm, wg_hbm, wu_hbm, wd_hbm, out_ref,
+               xg, hid, wg_buf, wu_buf, wd_buf, part, mate_out, mate_in, relay, from_x, from_y, x_mid,
+               wg_sem, wu_sem, wd_sem, send_sem, recv_sem, x_sem):
     me = lax.axis_index('tp')
     mate = me + 1 - 2 * lax.rem(me, 2)
     xpeer = me + 2 - 4 * lax.rem(me // 2, 2)
@@ -83,8 +84,9 @@
     side = [pl.ds(i * (width // quarters), width // quarters) for i in range(quarters)]
     pair = [[remote(mate_out.at[(g + 1) % 2, :, cols], mate_in.at[g, :, cols], mate) for cols in side]
             for g in range(groups)]
-    near_sx = [remote(part.at[1, span(0, c), :], from_x.at[span(0, c), :], xpeer) for c in chunks]
-    near_sy = [remote(part.at[1, span(PIECE, c), :], from_y.at[span(PIECE, c), :], ypeer) for c in chunks]
+    high, low = pl.ds(0, PIECE), pl.ds(PIECE, PIECE)
+    near_sx = [remote(part.at[1, high, cols], from_x.at[high, cols], xpeer) for cols in side]
+    near_sy = [remote(part.at[1, low, cols], from_y.at[low, cols], ypeer) for cols in side]
     diag_sx = [remote(part.at[2, span(0, c), :], relay.at[span(PIECE, c), :], xpeer) for c in chunks]
     diag_sy = [remote(part.at[2, span(PIECE, c), :], relay.at[span(0, c), :], ypeer) for c in chunks]
     far_sx = [remote(part.at[3, span(0, c), :], from_x.at[span(PIECE, c), :], xpeer) for c in chunks]
@@ -95,6 +97,8 @@
     far_x[0].start()
     far_y[0].start()
     own_mate.start()
+    mid_copy = pltpu.make_async_copy(xmid_hbm, x_mid, x_sem)
+    mid_copy.start()
     xg[pl.ds(0, ROWS), :] = xn_ref[...]
     own_mate.wait_recv()
 
@@ -127,11 +131,19 @@
             far_y[c].wait_recv()
         far_mate.start()
 
-    def send_near():
-        add_pair(1)
-        for c in chunks:
-            near_sx[c].start()
-            near_sy[c].start()
+    def send_near(i):
+        pair[1][i].wait_recv()
+
+        @pl.loop(0, ROWS // 8)
+        def _(r):
+            rows = pl.ds(pl.multiple_of(r * 8, 8), 8)
+            part[1, rows, side[i]] += mate_in[1, rows, side[i]]
+        near_sx[i].start()
+        near_sy[i].start()
+
+    def send_near_and_gather():
+        send_near(1)
+        gather_diag()
 
     def send_diag():
         add_pair(2)
@@ -144,8 +156,8 @@
             copy.wait_send()
 
     def start_diag():
-        send_near()
-        gather_diag()
+        send_near(2)
+        send_near(3)
         diag_mate.wait_recv()
 
     def start_far():
@@ -168,6 +180,8 @@
         (3, 0): start_far,
     }
     before_n = {
+        (1, n_steps - 4): lambda: send_near(0),
+        (1, n_steps - 2): send_near_and_gather,
         (3, 0): lambda: free_slot(1),
         (0, 0): lambda: free_slot(2),
         (0, n_steps // 2): lambda: add_pair(3),
@@ -232,10 +246,10 @@
 
 
     add_pair(0)
-    for c in chunks:
-        near_sx[c].wait_recv()
-        near_sy[c].wait_recv()
-    part[0] = part[0] + xmid_ref[...]
+    for copy in near_sx + near_sy:
+        copy.wait_recv()
+    mid_copy.wait()
+    part[0] = part[0] + x_mid[...]
     part[0, pl.ds(0, PIECE), :] += from_x[pl.ds(0, PIECE), :]
     part[0, pl.ds(PIECE, PIECE), :] += from_y[pl.ds(PIECE, PIECE), :]
     for c in chunks[1:]:
@@ -258,14 +272,14 @@
     h_tile, n_tile = 256, 512
     gu_slots, d_slots = 3, 3
     groups = num_tp // 2
-    copies = 8 + 4 * groups + 8 * (PIECE // SUB)
+    copies = 8 + 4 * groups + 8 + 6 * (PIECE // SUB)
     f32, bf16 = jnp.float32, jnp.bfloat16
     vmem = pl.BlockSpec(memory_space=pltpu.VMEM)
     hbm = pl.BlockSpec(memory_space=pl.ANY)
     return pl.pallas_call(
         functools.partial(mlp_kernel, num_tp),
         out_shape=jax.ShapeDtypeStruct((ROWS, width), bf16),
-        in_specs=[vmem, vmem, hbm, hbm, hbm],
+        in_specs=[vmem, hbm, hbm, hbm, hbm],
         out_specs=vmem,
         scratch_shapes=[
             pltpu.VMEM((num_tp * ROWS, width), bf16),
@@ -279,11 +293,13 @@
             pltpu.VMEM((ROWS, width), f32),
             pltpu.VMEM((ROWS, width), f32),
             pltpu.VMEM((ROWS, width), f32),
+            pltpu.VMEM((ROWS, width), f32),
             pltpu.SemaphoreType.DMA((gu_slots,)),
             pltpu.SemaphoreType.DMA((gu_slots,)),
             pltpu.SemaphoreType.DMA((d_slots,)),
             pltpu.SemaphoreType.DMA((copies,)),
             pltpu.SemaphoreType.DMA((copies,)),
+            pltpu.SemaphoreType.DMA,
         ],
         compiler_params=pltpu.CompilerParams(
             collective_id=0, has_side_effects=True, vmem_limit_bytes=67043328),
@@ -293,27 +309,23 @@
     )(xn_mid, x_mid, w_gate, w_up, w_down)
 
 
-def rope_tables(positions, head_dim):
-    half_dim = head_dim // 2
-    inv_freq = 10000.0 ** (-2.0 * jnp.arange(half_dim, dtype=jnp.float32) / head_dim)
-    angles = positions.astype(jnp.float32)[:, None] * inv_freq[None, :]
-    return jnp.cos(angles), jnp.sin(angles)
-
-
 TEAM = 8
 BLOCK = 128
-AHEAD = 4
-
-
-def attention_kernel(order, lens, hid_ref, ga_ref, gm_ref, cos_ref, sin_ref, wk_hbm, wv_hbm, wq_hbm, wo_hbm,
-                     kc_hbm, vc_hbm, xn_out, xmid_out, knew_out, vnew_out,
-                     w_buf, k_buf, v_buf, xn, q_lo, q_hi, o_lo, o_hi, k_row, v_row, squares,
-                     w_sem, k_sem, v_sem):
+AHEAD = 2
+WIDE = 2
+
+
+def attention_kernel(lens, row_ref, freq_ref, hid_ref, ga_ref, gm_ref, wk_hbm, wv_hbm, wq_hbm, wo_hbm,
+                     kc_hbm, vc_hbm, xn_out, xmid_hbm, knew_out, vnew_out,
+                     w_buf, k_buf, v_buf, xn, q_lo, q_hi, o_lo, o_hi, k_row, v_row, squares, cos_ref, sin_ref,
+                     x_mid, rank_row, order_smem, w_sem, k_sem, v_sem, x_sem, order_sem):
     num_rows, width = hid_ref.shape
     head_dim = wk_hbm.shape[1]
     half = head_dim // 2
     heads = wq_hbm.shape[1] // head_dim
-    tiles = wo_hbm.shape[1] // head_dim
+    tile_cols = WIDE * head_dim
+    steps = heads // WIDE
+    tiles = wo_hbm.shape[1] // tile_cols
     teams = num_rows // TEAM
     slots = k_buf.shape[0]
     w_slots = w_buf.shape[0]
@@ -321,27 +333,48 @@
     f32, bf16 = jnp.float32, jnp.bfloat16
 
     def tile_copy(src, tile, slot):
-        cols = pl.ds(pl.multiple_of(tile * head_dim, head_dim), head_dim)
+        cols = pl.ds(pl.multiple_of(tile * tile_cols, tile_cols), tile_cols)
         return pltpu.make_async_copy(src.at[:, cols], w_buf.at[slot], w_sem.at[slot])
 
-    def head_copy(head):
-        return tile_copy(wq_hbm, head, lax.rem(head + 2, w_slots))
+    def head_copy(step):
+        return tile_copy(wq_hbm, step, lax.rem(step + 1, w_slots))
 
     def out_copy(tile):
         return tile_copy(wo_hbm, tile, tile)
 
+    first = [pltpu.make_async_copy(wk_hbm, w_buf.at[0, :, pl.ds(0, head_dim)], w_sem.at[0]),
+             pltpu.make_async_copy(wv_hbm, w_buf.at[0, :, pl.ds(head_dim, head_dim)], w_sem.at[w_slots])]
+    for copy in first:
+        copy.start()
+    head_copy(jnp.int32(0)).start()
+
+    across = jnp.broadcast_to(row_ref[...].astype(f32), (num_rows, num_rows))
+    down = jnp.transpose(across)
+    row_id = lax.broadcasted_iota(jnp.int32, (num_rows, num_rows), 0)
+    col_id = lax.broadcasted_iota(jnp.int32, (num_rows, num_rows), 1)
+    is_ahead = (across < down) | ((across == down) & (col_id < row_id))
+    rank = jnp.sum(jnp.where(is_ahead, 1.0, 0.0), axis=1, keepdims=True)
+    placed = jnp.where(rank == col_id.astype(f32), row_id.astype(f32), 0.0)
+    rank_row[...] = jnp.sum(placed, axis=0, keepdims=True).astype(jnp.int32)
+    order_copy = pltpu.make_async_copy(rank_row, order_smem, order_sem)
+    order_copy.start()
+    angles = down * freq_ref[...]
+    cos_ref[...] = jnp.cos(angles)
+    sin_ref[...] = jnp.sin(angles)
+    order_copy.wait()
+
     def units_of(team):
-        longest = lens[order[team * TEAM + TEAM - 1]]
+        longest = lens[order_smem[0, team * TEAM + TEAM - 1]]
         return jnp.maximum((longest + BLOCK - 1) // BLOCK, 1)
 
     def key_copy(team, r, n):
         slot, span = lax.rem(team, slots), pl.ds(0, n * BLOCK)
-        return pltpu.make_async_copy(kc_hbm.at[order[team * TEAM + r], span, :],
+        return pltpu.make_async_copy(kc_hbm.at[order_smem[0, team * TEAM + r], span, :],
                                      k_buf.at[slot, r, span, :], k_sem.at[slot, r])
 
     def value_copy(team, r, n):
         slot, span = lax.rem(team, slots), pl.ds(0, n * BLOCK)
-        return pltpu.make_async_copy(vc_hbm.at[order[team * TEAM + r], span, :],
+        return pltpu.make_async_copy(vc_hbm.at[order_smem[0, team * TEAM + r], span, :],
                                      v_buf.at[slot, r, span, :], v_sem.at[slot, r])
 
     def fetch(team):
@@ -363,11 +396,6 @@
             inv = lax.rsqrt(jnp.mean(wide * wide, axis=-1, keepdims=True) + 1e-6)
             dst[rows, :] = (wide * inv * gain).astype(bf16)
 
-    first = [tile_copy(wk_hbm, 0, 0), tile_copy(wv_hbm, 0, 1)]
-    for copy in first:
-        copy.start()
-    for head in range(AHEAD - 2):
-        head_copy(jnp.int32(head)).start()
     normalise(hid_ref, ga_ref, xn)
 
     def rotate(lin):
@@ -375,40 +403,40 @@
         cos_t, sin_t = cos_ref[...], sin_ref[...]
         return low * cos_t - high * sin_t, high * cos_t + low * sin_t
 
-    first[0].wait()
-    head_copy(jnp.int32(AHEAD - 2)).start()
-    low, high = rotate(jnp.dot(xn[...], w_buf[0], preferred_element_type=f32))
+    for copy in first:
+        copy.wait()
+    head_copy(jnp.int32(1)).start()
+    both = jnp.dot(xn[...], w_buf[0], preferred_element_type=f32)
+    low, high = rotate(both[:, :head_dim])
     key = jnp.concatenate([low, high], axis=-1).astype(bf16)
     knew_out[...] = key
     k_row[...] = key.astype(f32)
-    first[1].wait()
-    head_copy(jnp.int32(AHEAD - 1)).start()
-    value = jnp.dot(xn[...], w_buf[1], preferred_element_type=f32).astype(bf16)
+    value = both[:, head_dim:].astype(bf16)
     vnew_out[...] = value
     v_row[...] = value.astype(f32)
 
-    early = range(slots - 1)
-
-    @pl.loop(0, heads)
-    def _(head):
-        head_copy(head).wait()
-
-        @pl.when(head + AHEAD < heads)
+    @pl.loop(0, steps)
+    def _(step):
+        head_copy(step).wait()
+
+        @pl.when(step + AHEAD < steps)
         def _():
-            head_copy(head + AHEAD).start()
-        for team in early:
-            @pl.when(head == heads - AHEAD + team)
+            head_copy(step + AHEAD).start()
+        for team in range(slots - 1):
+            @pl.when(step == steps - AHEAD + team)
             def _():
                 fetch(jnp.int32(team))
-        low, high = rotate(jnp.dot(xn[...], w_buf[lax.rem(head + 2, w_slots)], preferred_element_type=f32))
-        spots = pl.ds(head, num_rows, stride=heads)
-        q_lo[spots, :] = (low * head_dim ** -0.5).astype(bf16).astype(f32)
-        q_hi[spots, :] = (high * head_dim ** -0.5).astype(bf16).astype(f32)
+        lin = jnp.dot(xn[...], w_buf[lax.rem(step + 1, w_slots)], preferred_element_type=f32)
+        for i in range(WIDE):
+            low, high = rotate(lin[:, i * head_dim:(i + 1) * head_dim])
+            spots = pl.ds(step * WIDE + i, num_rows, stride=heads)
+            q_lo[spots, :] = (low * head_dim ** -0.5).astype(bf16).astype(f32)
+            q_hi[spots, :] = (high * head_dim ** -0.5).astype(bf16).astype(f32)
 
     def attend(team, n):
         slot = lax.rem(team, slots)
         size = n * BLOCK
-        rows = [order[team * TEAM + r] for r in range(TEAM)]
+        rows = [order_smem[0, team * TEAM + r] for r in range(TEAM)]
         spans = [pl.ds(pl.multiple_of(row * heads, heads), heads) for row in rows]
         for r in range(TEAM):
             key_copy(team, r, n).wait()
@@ -435,15 +463,16 @@
             o_lo[spans[r], :] = mixed[:, :half]
             o_hi[spans[r], :] = mixed[:, half:]
 
-    share = tiles // teams
+    share = teams // tiles
 
     @pl.loop(0, teams)
     def _(team):
         @pl.when(team + slots - 1 < teams)
         def _():
             fetch(team + slots - 1)
-        for part in range(share):
-            out_copy(team * share + part).start()
+        @pl.when(lax.rem(team, share) == 0)
+        def _():
+            out_copy(team // share).start()
         units = units_of(team)
         for n in range(1, max_units + 1):
             @pl.when(units == n)
@@ -456,14 +485,19 @@
         xn[:, pl.ds(head * head_dim + half, half)] = o_hi[spots, :].astype(bf16)
     squares[...] = jnp.zeros_like(squares)
 
+    def mid_copy(tile):
+        cols = pl.ds(pl.multiple_of(tile * tile_cols, tile_cols), tile_cols)
+        return pltpu.make_async_copy(x_mid.at[:, cols], xmid_hbm.at[:, cols], x_sem.at[tile])
+
     @pl.loop(0, tiles)
     def _(tile):
         out_copy(tile).wait()
-        cols = pl.ds(pl.multiple_of(tile * head_dim, head_dim), head_dim)
+        cols = pl.ds(pl.multiple_of(tile * tile_cols, tile_cols), tile_cols)
         mixed = hid_ref[:, cols].astype(f32) + jnp.dot(xn[...], w_buf[tile], preferred_element_type=f32)
-        xmid_out[:, cols] = mixed
+        x_mid[:, cols] = mixed
+        mid_copy(tile).start()
         mixed = mixed * mixed
-        squares[...] += mixed[:, :half] + mixed[:, half:]
+        squares[...] += sum(mixed[:, i * half:(i + 1) * half] for i in range(tile_cols // half))
 
     gain = 1.0 + gm_ref[...].astype(f32)[None, :]
 
@@ -471,7 +505,10 @@
     def _(i):
         rows = pl.ds(pl.multiple_of(i * 16, 16), 16)
         inv = lax.rsqrt(jnp.sum(squares[rows, :], axis=-1, keepdims=True) * (1.0 / width) + 1e-6)
-        xn_out[rows, :] = (xmid_out[rows, :] * inv * gain).astype(bf16)
+        xn_out[rows, :] = (x_mid[rows, :] * inv * gain).astype(bf16)
+
+    for tile in range(tiles):
+        mid_copy(jnp.int32(tile)).wait()
 
 
 def attention_block(hidden_in, k_cache, v_cache, cache_len, norm_attn, norm_mlp, w_q, w_k, w_v, w_o):
@@ -479,13 +516,8 @@
     head_dim = w_k.shape[1]
     half = head_dim // 2
     heads = w_q.shape[1] // head_dim
-    cos_t, sin_t = rope_tables(cache_len, head_dim)
-    spot = jnp.arange(num_rows, dtype=jnp.int32)
-    ahead = (cache_len[None, :] < cache_len[:, None]) | (
-        (cache_len[None, :] == cache_len[:, None]) & (spot[None, :] < spot[:, None]))
-    rank = jnp.sum(ahead.astype(jnp.int32), axis=1)
-    order = jnp.sum(jnp.where(rank[:, None] == spot[None, :], spot[:, None], 0), axis=0)
-    slots, w_slots = 3, w_o.shape[1] // head_dim
+    inv_freq = (10000.0 ** (-2.0 * np.arange(half) / head_dim)).astype(np.float32)
+    slots, tiles = 3, w_o.shape[1] // (WIDE * head_dim)
     f32, bf16 = jnp.float32, jnp.bfloat16
     vmem = pl.BlockSpec(memory_space=pltpu.VMEM)
     smem = pl.BlockSpec(memory_space=pltpu.SMEM)
@@ -495,10 +527,10 @@
         attention_kernel,
         out_shape=[jax.ShapeDtypeStruct((num_rows, width), bf16), jax.ShapeDtypeStruct((num_rows, width), f32),
                    jax.ShapeDtypeStruct((num_rows, head_dim), bf16), jax.ShapeDtypeStruct((num_rows, head_dim), bf16)],
-        in_specs=[smem, smem, vmem, vmem, vmem, vmem, vmem, hbm, hbm, hbm, hbm, hbm, hbm],
-        out_specs=[vmem] * 4,
+        in_specs=[smem, vmem, vmem, vmem, vmem, vmem, hbm, hbm, hbm, hbm, hbm, hbm],
+        out_specs=[vmem, hbm, vmem, vmem],
         scratch_shapes=[
-            pltpu.VMEM((w_slots, width, head_dim), bf16),
+            pltpu.VMEM((tiles, width, WIDE * head_dim), bf16),
             pltpu.VMEM(team_shape, bf16),
             pltpu.VMEM(team_shape, bf16),
             pltpu.VMEM((num_rows, width), bf16),
@@ -509,15 +541,22 @@
             pltpu.VMEM((num_rows, head_dim), f32),
             pltpu.VMEM((num_rows, head_dim), f32),
             pltpu.VMEM((num_rows, half), f32),
-            pltpu.SemaphoreType.DMA((w_slots,)),
+            pltpu.VMEM((num_rows, half), f32),
+            pltpu.VMEM((num_rows, half), f32),
+            pltpu.VMEM((num_rows, width), f32),
+            pltpu.VMEM((1, num_rows), jnp.int32),
+            pltpu.SMEM((1, num_rows), jnp.int32),
+            pltpu.SemaphoreType.DMA((tiles + 1,)),
             pltpu.SemaphoreType.DMA((slots, TEAM)),
             pltpu.SemaphoreType.DMA((slots, TEAM)),
+            pltpu.SemaphoreType.DMA((tiles,)),
+            pltpu.SemaphoreType.DMA,
         ],
         compiler_params=pltpu.CompilerParams(vmem_limit_bytes=67043328),
         cost_estimate=pl.CostEstimate(flops=4 * num_rows * width * width, bytes_accessed=4 * width * width,
                                       transcendentals=0),
         name='attention_block',
-    )(order, cache_len, hidden_in, norm_attn, norm_mlp, cos_t, sin_t, w_k, w_v, w_q, w_o,
+    )(cache_len, cache_len[None, :], inv_freq[None, :], hidden_in, norm_attn, norm_mlp, w_k, w_v, w_q, w_o,
       k_cache, v_cache)
 
 

time: 166 us -> 159 us (0.958)
  other arithmetic: 3.22 us -> 0 us
  Pallas kernels: 159 us -> 157 us
    pallas_call x1, Pallas kernels: 48 us -> 46.1 us  [attention_block(): pl.pallas_call(attention_kernel, out_shape=[jax.ShapeDtypeStruct((num_row...]
where the time goes in v3:
time: 159 us
  Pallas kernels  157 us (99%)
  local copies, waits for them, and re-layouts  2.29 us (1%)
    pallas_call x1, Pallas kernels, exchange_mlp(): pl.pallas_call(functools.partial(mlp_kernel, num_tp), out_shape=jax.Shape...  110 us
    pallas_call x1, Pallas kernels, attention_block(): pl.pallas_call(attention_kernel, out_shape=[jax.ShapeDtypeStruct((num_row...  46.1 us

profile of v3, /device:TPU:0, one launch (start us, length us, event | category | flops | bytes accessed | tf_op | source)
XLA Modules:
  0.0 159.5 jit_solution(4141067647728554621)
XLA Ops:
  0.6 46.1 %attention_block.1 = (bf16[128,4096]{1,0:T(8,128)(2,1)}, f32[128,4096]{1,0:T(8,128)}, bf16[128,256]{1,0:T(8,128)(2,1)}, bf16[128,256]{1,0:T(8,128)(2,1)}) custom-call(s32[128]{0:T(128)} %lens.1, s32[1,128]{1,0:T(1,128)} %bitcast.1, f32[1,128]{1,0:T(1,128)} %constant.2.clone.freq_ref, bf16[128,4096]{1,0:T(8,128)(2,1)} %hid_ref.1, bf16[4096]{0:T(1024)(128)(2,1)} %ga_ref.1, ...), custom_call_target="tpu_custom_call" | custom-call | flops 8589934592 | bytes 67108864 | tf_op jit(solution)/shard_map/attention_block/pallas_call | solution.py:526
  46.8 110.4 %exchange_mlp.1 = bf16[128,4096]{1,0:T(8,128)(2,1)} custom-call(bf16[128,4096]{1,0:T(8,128)(2,1)} %get-tuple-element.7.xn_ref, f32[128,4096]{1,0:T(8,128)} %get-tuple-element.8.xmid_hbm, bf16[4096,2048]{1,0:T(8,128)(2,1)} %wg_hbm.1, bf16[4096,2048]{1,0:T(8,128)(2,1)} %wu_hbm.1, bf16[2048,4096]{1,0:T(8,128)(2,1)} %wd_hbm.1), custom_call_target="tpu_custom_call" | custom-call | flops 51539607552 | bytes 201326592 | tf_op jit(solution)/shard_map/exchange_mlp/pallas_call | solution.py:279
  157.2 2.3 %copy.18 = bf16[128,4096]{1,0:T(8,128)(2,1)} copy(bf16[128,4096]{1,0:T(8,128)(2,1)} %exchange_mlp.1) | data formatting | bytes 2097152
